TPU v7x, 32 devices: a whole 2x2x4 slice. The times are simulated.
32 devices in a mesh: blk: 32 (over z, y, x, core).
Axes of the slice: x: 2, y: 2, z: 4, core: 2. Of those that a mesh axis runs over, the one named last changes fastest.
Arguments:
- panel_left: bfloat16 [64, 64, 2048], P('blk'), may hold values from -0.75 to 0.75
- panel_right: bfloat16 [64, 64, 2048], P('blk'), may hold values from -0.125 to 0.125
- ranks: int32 [64], P('blk'), may hold values from 1 to 64
- rhs: float32 [64, 64, 2048], P('blk'), may hold values from -6 to 6
- pivot_left: bfloat16 [2048, 64], P('blk'), may hold values from -0.75 to 0.75
- pivot_right: bfloat16 [2048, 64], P('blk'), may hold values from -6 to 6
- finished: float32 [2048, 64], P('blk'), may hold values from -6 to 6
- pivot_rhs: float32 [2048, 64], P('blk'), may hold values from -6 to 6
- diag_inverse: float32 [2048, 2048], P('blk'), as said below
Outputs:
- new_left: bfloat16 [64, 64, 2048], P('blk')
- new_rhs: float32 [64, 64, 2048], P('blk')
- next_solution: float32 [2048, 64], P('blk')
Inputs may be any that keep to these rules, and one draw needn't show every extreme that they name: diag_inverse is lower triangular with diagonal entries between 1 and 2.
All inputs are finite; a program needn't handle non-finite values.
Results may differ from a plain program's by a relative error of at most 0.0049.
Values sent between devices are 32-bit elements; how exact they have to be, the bound alone decides.
A program may use at most 64 MiB of HBM per device.

v0:
```python
import jax
import jax.numpy as jnp
from jax import lax
from jax.sharding import PartitionSpec as P

HIGH = lax.Precision.HIGHEST


def shards(
    panel_left, panel_right, ranks, rhs, pivot_left, pivot_right, finished, pivot_rhs, diag_inverse
):
    kmax = panel_left.shape[1]
    mask = (jnp.arange(kmax, dtype=jnp.int32)[None, :] < ranks[:, None]).astype(jnp.bfloat16)
    left_m = panel_left * mask[:, :, None]
    right_wide = (panel_right * mask[:, :, None]).astype(jnp.float32)
    pivot_wide = pivot_right.astype(jnp.float32)
    right_piece = lax.all_gather(pivot_wide, "blk", axis=0, tiled=True)
    solved_piece = lax.all_gather(finished, "blk", axis=0, tiled=True)
    gram_sum = jnp.einsum("rkn,nj->rkj", right_wide, right_piece, precision=HIGH)
    proj_sum = jnp.einsum("rkn,nj->rkj", right_wide, solved_piece, precision=HIGH)
    pivot_sum = jnp.dot(right_piece.T, solved_piece, precision=HIGH)
    new_left = jnp.einsum(
        "rkj,rkn->rjn", gram_sum.astype(jnp.bfloat16), left_m, preferred_element_type=jnp.float32
    ).astype(jnp.bfloat16)
    new_rhs = rhs - jnp.einsum("rkj,rkn->rjn", proj_sum, left_m.astype(jnp.float32), precision=HIGH)
    pivot_new = pivot_rhs - jnp.dot(pivot_left.astype(jnp.float32), pivot_sum, precision=HIGH)
    next_solution = jnp.dot(
        diag_inverse, lax.all_gather(pivot_new, "blk", axis=0, tiled=True), precision=HIGH
    )
    return (new_left, new_rhs, next_solution)


def solution(mesh):
    in_specs = (
        P("blk", None, None),
        P("blk", None, None),
        P("blk"),
        P("blk", None, None),
        P("blk", None),
        P("blk", None),
        P("blk", None),
        P("blk", None),
        P("blk", None),
    )
    out_specs = (P("blk", None, None), P("blk", None, None), P("blk", None))
    return jax.shard_map(shards, mesh=mesh, in_specs=in_specs, out_specs=out_specs, check_vma=False)
```

profile of v0, /device:TPU:0, one launch (start us, length us, event | category | flops | bytes accessed | tf_op | source)
XLA Modules:
  0.0 138.4 jit_solution(10801241229913180033)
XLA Ops:
  0.6 0.0 copy-start
  0.6 0.8 compare_convert_fusion
  1.4 0.7 convert_element_type.20
  2.2 0.0 copy-start.1
  2.2 46.3 %all_gather.9 = f32[2048,64]{1,0:T(8,128)S(1)} all-gather(f32[64,64]{1,0:T(8,128)S(1)} %convert_element_type.20), channel_id=1, replica_groups=mesh['blk'=32] {'blk'}, dimensions={0}, use_global_device_ids=true | all-gather | bytes 540672 | tf_op jit(solution)/shard_map/all_gather | solution.py:17
  48.5 0.0 copy-done.1
  48.5 0.0 copy-start.2
  48.5 1.1 convolution_convert_fusion.1
  49.5 0.0 copy-done.2
  49.5 0.0 copy-start.4
  49.5 1.1 convolution_convert_fusion
  50.7 0.0 copy-done.4
  50.7 39.5 %all_gather.10 = f32[2048,64]{1,0:T(8,128)S(1)} all-gather(f32[64,64]{1,0:T(8,128)S(1)} %copy-done.4), channel_id=1, replica_groups=mesh['blk'=32] {'blk'}, dimensions={0}, use_global_device_ids=true | all-gather | bytes 540672 | tf_op jit(solution)/shard_map/all_gather | solution.py:18
  90.2 1.9 %fusion.12 = f32[64,64]{1,0:T(8,128)S(1)} fusion(f32[2048,64]{1,0:T(8,128)S(1)} %all_gather.9, f32[2048,64]{1,0:T(8,128)S(1)} %all_gather.10), kind=kOutput, calls=%fused_computation.18 | convolution fusion | flops 100663296 | bytes 1064960 | tf_op jit(solution)/shard_map/dot_general | solution.py:21
  92.1 0.0 copy-start.5
  92.1 0.0 copy-start.6
  92.1 0.0 copy-start.3
  92.1 1.1 fusion.1
  93.2 0.0 copy-done.5
  93.2 0.0 copy-done.6
  93.2 0.1 fusion
  93.3 0.0 copy-done.3
  93.3 1.6 %convolution_subtract_fusion = f32[2,64,2048]{2,1,0:T(8,128)} fusion(f32[2,64,2048]{2,1,0:T(8,128)S(1)} %copy-done.3, f32[2,64,64]{1,2,0:T(8,128)S(1)} %fusion.1, bf16[2,64,2048]{2,1,0:T(8,128)(2,1)S(1)} %copy-done.2, bf16[2,64]{1,0:T(2,128)(2,1)S(1)} %compare_convert_fusion), kind=kOutput, calls=%fused_computation | convolution fusion | flops 201850880 | bytes 2654464 | tf_op jit(solution)/shard_map/rkj,rkn->rjn/dot_general | solution.py:25
  95.0 40.9 %all_gather.11 = f32[2048,64]{1,0:T(8,128)S(1)} all-gather(f32[64,64]{1,0:T(8,128)S(1)} %fusion), channel_id=1, replica_groups=mesh['blk'=32] {'blk'}, dimensions={0}, use_global_device_ids=true | all-gather | bytes 540672 | tf_op jit(solution)/shard_map/all_gather | solution.py:28
  135.8 0.0 copy-done
  135.9 1.8 %convolution_bitcast_fusion = f32[64,64]{0,1:T(8,128)S(1)} fusion(f32[2048,64]{1,0:T(8,128)S(1)} %all_gather.11, f32[64,2048]{1,0:T(8,128)S(1)} %copy-done), kind=kOutput, calls=%fused_computation.3 | convolution fusion | flops 100663296 | bytes 1064960 | tf_op jit(solution)/shard_map/dot_general | solution.py:27
  137.7 0.7 copy.12
Async XLA Ops:
  0.6 135.2 %copy-start = (f32[64,2048]{1,0:T(8,128)S(1)}, f32[64,2048]{1,0:T(8,128)}, u32[]{:S(2)}) copy-start(f32[64,2048]{1,0:T(8,128)} %param.17) | copy-start | bytes 1572868
  2.2 46.3 %copy-start.1 = (bf16[2,64,2048]{2,1,0:T(8,128)(2,1)S(1)}, bf16[2,64,2048]{2,1,0:T(8,128)(2,1)}, u32[]{:S(2)}) copy-start(bf16[2,64,2048]{2,1,0:T(8,128)(2,1)} %param.10) | copy-start | bytes 1572868
  48.5 1.1 copy-start.2
  49.5 1.2 copy-start.4
  92.1 1.1 copy-start.5
  92.1 1.1 copy-start.6
  92.1 1.2 copy-start.3
where the time goes:
time: 139 us; the launch traced here: 138 us
  blocking collectives  127 us (91%)
  matrix products  8.74 us (6%)
  other arithmetic  1.5 us (1%)
    all_gather x1, blocking collectives, shards(): right_piece = lax.all_gather(pivot_wide, 'blk', axis=0, tiled=True)  46.3 us
    all_gather x1, blocking collectives, shards(): lax.all_gather(pivot_new, 'blk', axis=0, tiled=True)  40.9 us
    all_gather x1, blocking collectives, shards(): solved_piece = lax.all_gather(finished, 'blk', axis=0, tiled=True)  39.5 us

commit v1 on v0

v1 whole, which is shorter than its diff:
```python
import functools

import jax
import jax.numpy as jnp
from jax import lax
from jax.experimental import pallas as pl
from jax.experimental.pallas import tpu as pltpu
from jax.sharding import PartitionSpec as P

MESH = pl.DeviceIdType.MESH
F32 = jnp.float32
BF16 = jnp.bfloat16


def factors(n):
    side = 1
    while (side * 2) ** 3 * 2 <= n and n % (2 * (side * 2) ** 2) == 0:
        side *= 2
    return n // (2 * side * side), side


def gather_kernel(
    n,
    right_any,
    diag_any,
    pr_ref,
    fin_ref,
    pl_ref,
    prhs_ref,
    prod_ref,
    next_ref,
    buf,
    right_v,
    diag_v,
    in_sem,
    send_sem,
    recv_sem,
):
    deep, side = factors(n)
    me = lax.axis_index("blk")
    core = me % 2
    dx = (me // 2) % side
    dy = (me // (2 * side)) % side
    z = me // (2 * side * side)
    s1 = 2 + core * (2 * side - 2)
    s2 = 2 * side - core * (2 * side - 2)
    f = dx + core * (dy - dx)
    g = dy + core * (dx - dy)

    def block(zz, ff, gg, cc=core):
        return zz * (2 * side * side) + ff * s1 + gg * s2 + cc

    load_right = pltpu.make_async_copy(right_any, right_v, in_sem.at[0])
    load_diag = pltpu.make_async_copy(diag_any, diag_v, in_sem.at[1])
    load_right.start()
    load_diag.start()
    half = pr_ref.shape[1]
    buf[0, me] = jnp.concatenate([pr_ref[...].astype(F32), fin_ref[...]], axis=1)
    buf[1, me] = jnp.concatenate([pl_ref[...].astype(F32), prhs_ref[...]], axis=1)

    def around(digit, size):
        order = sorted(range(1, size), key=lambda d: min(d, size - d))
        return [(digit + d) % size for d in order]

    zs, fs, gs = around(z, deep), around(f, side), around(g, side)
    partner = me + 1 - 2 * core
    z_to = [block(zz, f, g) for zz in zs]
    f_to = [block(z, ff, g) for ff in fs]
    g_to = [block(z, f, gg) for gg in gs]

    barrier = pltpu.get_barrier_semaphore()
    everyone = z_to + f_to + g_to + [partner]
    for peer in everyone:
        pl.semaphore_signal(barrier, inc=1, device_id=(peer,), device_id_type=MESH)
    pl.semaphore_wait(barrier, len(everyone))

    sent = []

    def copy(p, blk, to, slot):
        return pltpu.make_async_remote_copy(
            src_ref=buf.at[p, blk],
            dst_ref=buf.at[p, blk],
            send_sem=send_sem.at[p, slot],
            recv_sem=recv_sem.at[p, blk],
            device_id=(to,),
            device_id_type=MESH,
        )

    counts = [0, 0]

    def send(p, blk, to):
        c = copy(p, blk, to, counts[p])
        counts[p] += 1
        c.start()
        sent.append(c)

    def arrive(p, blk):
        copy(p, blk, partner, 0).wait_recv()

    def forward(p, blk, targets):
        for to in targets:
            send(p, blk, to)

    def own(p):
        forward(p, me, z_to + f_to + g_to + [partner])

    def stage_z(p):
        for zz in zs:
            blk = block(zz, f, g)
            arrive(p, blk)
            forward(p, blk, f_to + g_to + [partner])

    def stage_f(p):
        for zz in [z] + zs:
            for ff in fs:
                blk = block(zz, ff, g)
                arrive(p, blk)
                forward(p, blk, g_to + [partner])

    def stage_g(p):
        for ff in [f] + fs:
            for zz in [z] + zs:
                for gg in gs:
                    blk = block(zz, ff, gg)
                    arrive(p, blk)
                    forward(p, blk, [partner])

    def stage_core(p):
        for gg in [g] + gs:
            for ff in [f] + fs:
                for zz in [z] + zs:
                    blk = zz * (2 * side * side) + ff * s1 + gg * s2 + 1 - core
                    arrive(p, blk)

    own(0)
    own(1)
    stage_z(0)
    stage_f(0)
    stage_z(1)
    stage_g(0)
    stage_f(1)
    stage_core(0)

    rows = n * buf.shape[2]
    solved = buf[0].reshape(rows, 2 * half).astype(BF16)
    load_right.wait()
    tiles, kmax, width = right_v.shape
    prod_ref[...] = jnp.dot(right_v[...].reshape(tiles * kmax, width), solved, preferred_element_type=F32)
    cross = lax.dot_general(solved, solved, (((0,), (0,)), ((), ())), preferred_element_type=F32)
    at_row = lax.broadcasted_iota(jnp.int32, cross.shape, 0)
    at_lane = lax.broadcasted_iota(jnp.int32, cross.shape, 1)
    weight = jnp.where((at_row < half) & (at_lane >= half), cross, 0.0).astype(BF16)
    load_diag.wait()

    stage_g(1)
    stage_core(1)
    both = buf[1].reshape(rows, 2 * half)
    update = jnp.dot(both.astype(BF16), weight, preferred_element_type=F32)
    pivot_new = (both - update).astype(BF16)
    answer = jnp.dot(diag_v[...].astype(BF16), pivot_new, preferred_element_type=F32)
    next_ref[...] = answer[:, half:]
    for c in sent:
        c.wait_send()


def tile_kernel(ranks_ref, prod_ref, left_ref, rhs_ref, next_in, nl_ref, nr_ref, next_out):
    t = pl.program_id(0)
    kmax = left_ref.shape[1]
    half = nl_ref.shape[1]
    rank = ranks_ref[t]
    prod = prod_ref[...]
    prod = jnp.where(lax.broadcasted_iota(jnp.int32, prod.shape, 0) < rank, prod, 0.0)
    coef = prod.T.astype(BF16)
    left = left_ref[0]
    keep = lax.broadcasted_iota(jnp.int32, left.shape, 0) < rank
    left_m = jnp.where(keep, left, jnp.zeros_like(left))
    out = jnp.dot(coef, left_m, preferred_element_type=F32)
    nl_ref[0] = out[:half].astype(nl_ref.dtype)
    nr_ref[0] = rhs_ref[0] - out[half:]
    next_out[...] = next_in[...]


def solution(mesh):
    n = mesh.shape["blk"]

    def shards(panel_left, panel_right, ranks, rhs, pivot_left, pivot_right, finished, pivot_rhs, diag_inverse):
        tiles, kmax, width = panel_left.shape
        rows, half = finished.shape
        vmem = pl.BlockSpec(memory_space=pltpu.VMEM)
        hbm = pl.BlockSpec(memory_space=pl.ANY)
        deep, side = factors(n)
        steps = (deep - 1) + deep * (side - 1) + deep * side * (side - 1) + deep * side * side
        prod, nxt = pl.pallas_call(
            functools.partial(gather_kernel, n),
            out_shape=(
                jax.ShapeDtypeStruct((tiles * kmax, 2 * half), F32),
                jax.ShapeDtypeStruct((rows, half), F32),
            ),
            in_specs=[hbm, hbm, vmem, vmem, vmem, vmem],
            out_specs=(vmem, vmem),
            scratch_shapes=[
                pltpu.VMEM((2, n, rows, 2 * half), F32),
                pltpu.VMEM(panel_right.shape, BF16),
                pltpu.VMEM(diag_inverse.shape, F32),
                pltpu.SemaphoreType.DMA((2,)),
                pltpu.SemaphoreType.DMA((2, steps)),
                pltpu.SemaphoreType.DMA((2, n)),
            ],
            compiler_params=pltpu.CompilerParams(
                collective_id=0, has_side_effects=True, vmem_limit_bytes=32 * 1024 * 1024
            ),
        )(panel_right, diag_inverse, pivot_right, finished, pivot_left, pivot_rhs)

        cut = 2 if width % 256 == 0 else 1
        chunk = width // cut
        new_left, new_rhs, next_solution = pl.pallas_call(
            tile_kernel,
            grid=(tiles, cut),
            out_shape=(
                jax.ShapeDtypeStruct((tiles, half, width), BF16),
                jax.ShapeDtypeStruct((tiles, half, width), F32),
                jax.ShapeDtypeStruct((rows, half), F32),
            ),
            in_specs=[
                pl.BlockSpec(memory_space=pltpu.SMEM),
                pl.BlockSpec((kmax, 2 * half), lambda t, w: (t, 0)),
                pl.BlockSpec((1, kmax, chunk), lambda t, w: (t, 0, w)),
                pl.BlockSpec((1, half, chunk), lambda t, w: (t, 0, w)),
                pl.BlockSpec((rows, half), lambda t, w: (0, 0)),
            ],
            out_specs=(
                pl.BlockSpec((1, half, chunk), lambda t, w: (t, 0, w)),
                pl.BlockSpec((1, half, chunk), lambda t, w: (t, 0, w)),
                pl.BlockSpec((rows, half), lambda t, w: (0, 0)),
            ),
        )(ranks, prod, panel_left, rhs, nxt)
        return new_left, new_rhs, next_solution

    in_specs = (
        P("blk", None, None),
        P("blk", None, None),
        P("blk"),
        P("blk", None, None),
        P("blk", None),
        P("blk", None),
        P("blk", None),
        P("blk", None),
        P("blk", None),
    )
    out_specs = (P("blk", None, None), P("blk", None, None), P("blk", None))
    return jax.shard_map(shards, mesh=mesh, in_specs=in_specs, out_specs=out_specs, check_vma=False)
```

time: 139 us -> 35 us (0.25)
  the two profiles are of different devices: /device:TPU:0 before, /device:TPU:5 now
where the time goes in v1:
time: 35 us; the launch traced here: 34.5 us
  Pallas kernels  27.5 us (79%)
  local copies, waits for them, and re-layouts  6.26 us (18%)
  between operations  0.66 us (2%)
    pallas_call x1, Pallas kernels, shards(): pl.pallas_call(functools.partial(gather_kernel, n), out_shape=(jax.ShapeD...  23.4 us
    unnamed x16, local copies, waits for them, and re-layouts  6.26 us
    pallas_call x1, Pallas kernels, shards(): pl.pallas_call(tile_kernel, grid=(tiles, cut), out_shape=(jax.ShapeDtypeS...  4.11 us

profile of v1, /device:TPU:5, one launch (start us, length us, event | category | flops | bytes accessed | tf_op | source)
XLA Modules:
  0.0 34.5 jit_solution(3791330366150681854)
XLA Ops:
  0.6 0.0 copy-start
  0.6 1.0 %copy-done = bf16[2,64,2048]{2,1,0:T(8,128)(2,1)S(1)} copy-done((bf16[2,64,2048]{2,1,0:T(8,128)(2,1)S(1)}, bf16[2,64,2048]{2,1,0:T(8,128)(2,1)}, u32[]{:S(2)}) %copy-start) | copy-done | bytes 524312
  1.7 0.0 copy-start.1
  1.7 1.0 %copy-done.1 = f32[64,2048]{1,0:T(8,128)S(1)} copy-done((f32[64,2048]{1,0:T(8,128)S(1)}, f32[64,2048]{1,0:T(8,128)}, u32[]{:S(2)}) %copy-start.1) | copy-done | bytes 524312
  2.7 0.0 copy-start.3
  2.7 0.8 %copy-done.3 = f32[64,64]{1,0:T(8,128)S(1)} copy-done((f32[64,64]{1,0:T(8,128)S(1)}, f32[64,64]{1,0:T(8,128)}, u32[]{:S(2)}) %copy-start.3) | copy-done | bytes 16408
  3.5 0.0 copy-start.4
  3.5 0.8 %copy-done.4 = f32[64,64]{1,0:T(8,128)S(1)} copy-done((f32[64,64]{1,0:T(8,128)S(1)}, f32[64,64]{1,0:T(8,128)}, u32[]{:S(2)}) %copy-start.4) | copy-done | bytes 16408
  4.2 0.0 copy-start.6
  4.2 0.7 %copy-done.6 = bf16[64,64]{1,0:T(8,128)(2,1)S(1)} copy-done((bf16[64,64]{1,0:T(8,128)(2,1)S(1)}, bf16[64,64]{1,0:T(8,128)(2,1)}, u32[]{:S(2)}) %copy-start.6) | copy-done | bytes 8216
  5.0 0.0 copy-start.7
  5.0 0.7 %copy-done.7 = bf16[64,64]{1,0:T(8,128)(2,1)S(1)} copy-done((bf16[64,64]{1,0:T(8,128)(2,1)S(1)}, bf16[64,64]{1,0:T(8,128)(2,1)}, u32[]{:S(2)}) %copy-start.7) | copy-done | bytes 8216
  5.7 23.4 %shard_map.112 = (f32[128,128]{1,0:T(8,128)S(1)}, f32[64,64]{1,0:T(8,128)S(1)}) custom-call(bf16[2,64,2048]{2,1,0:T(8,128)(2,1)S(1)} %copy-done, f32[64,2048]{1,0:T(8,128)S(1)} %copy-done.1, bf16[64,64]{1,0:T(8,128)(2,1)S(1)} %copy-done.6, f32[64,64]{1,0:T(8,128)S(1)} %copy-done.3, bf16[64,64]{1,0:T(8,128)(2,1)S(1)} %copy-done.7, f32[64,64]{1,0:T(8,128)S(1)} %copy-done.4), custom_call_target="tpu_custom_call" | custom-call | tf_op jit(solution)/shard_map/pallas_call | solution.py:193
  29.1 0.0 copy-start.2
  29.1 0.6 %copy-done.2 = f32[128,128]{1,0:T(8,128)} copy-done((f32[128,128]{1,0:T(8,128)}, f32[128,128]{1,0:T(8,128)S(1)}, u32[]{:S(2)}) %copy-start.2) | copy-done | bytes 65560
  29.7 0.0 copy-start.5
  29.7 0.6 %copy-done.5 = f32[64,64]{1,0:T(8,128)} copy-done((f32[64,64]{1,0:T(8,128)}, f32[64,64]{1,0:T(8,128)S(1)}, u32[]{:S(2)}) %copy-start.5) | copy-done | bytes 16408
  30.3 4.1 %shard_map.113 = (bf16[2,64,2048]{2,1,0:T(8,128)(2,1)}, f32[2,64,2048]{2,1,0:T(8,128)}, f32[64,64]{1,0:T(8,128)}) custom-call(s32[2]{0:T(128)} %ranks_ref.1, f32[128,128]{1,0:T(8,128)} %copy-done.2, bf16[2,64,2048]{2,1,0:T(8,128)(2,1)} %left_ref.1, f32[2,64,2048]{2,1,0:T(8,128)} %rhs_ref.1, f32[64,64]{1,0:T(8,128)} %copy-done.5), custom_call_target="tpu_custom_call" | custom-call | tf_op jit(solution)/shard_map/pallas_call | solution.py:216
Async XLA Ops:
  0.6 1.0 %copy-start = (bf16[2,64,2048]{2,1,0:T(8,128)(2,1)S(1)}, bf16[2,64,2048]{2,1,0:T(8,128)(2,1)}, u32[]{:S(2)}) copy-start(bf16[2,64,2048]{2,1,0:T(8,128)(2,1)} %right_any.1) | copy-start | bytes 1572868
  1.7 1.0 %copy-start.1 = (f32[64,2048]{1,0:T(8,128)S(1)}, f32[64,2048]{1,0:T(8,128)}, u32[]{:S(2)}) copy-start(f32[64,2048]{1,0:T(8,128)} %diag_any.1) | copy-start | bytes 1572868
  2.7 0.8 %copy-start.3 = (f32[64,64]{1,0:T(8,128)S(1)}, f32[64,64]{1,0:T(8,128)}, u32[]{:S(2)}) copy-start(f32[64,64]{1,0:T(8,128)} %fin_ref.1) | copy-start | bytes 49156
  3.5 0.8 %copy-start.4 = (f32[64,64]{1,0:T(8,128)S(1)}, f32[64,64]{1,0:T(8,128)}, u32[]{:S(2)}) copy-start(f32[64,64]{1,0:T(8,128)} %prhs_ref.1) | copy-start | bytes 49156
  4.2 0.7 %copy-start.6 = (bf16[64,64]{1,0:T(8,128)(2,1)S(1)}, bf16[64,64]{1,0:T(8,128)(2,1)}, u32[]{:S(2)}) copy-start(bf16[64,64]{1,0:T(8,128)(2,1)} %pr_ref.1) | copy-start | bytes 24580
  5.0 0.7 %copy-start.7 = (bf16[64,64]{1,0:T(8,128)(2,1)S(1)}, bf16[64,64]{1,0:T(8,128)(2,1)}, u32[]{:S(2)}) copy-start(bf16[64,64]{1,0:T(8,128)(2,1)} %pl_ref.1) | copy-start | bytes 24580
  29.1 0.6 %copy-start.2 = (f32[128,128]{1,0:T(8,128)}, f32[128,128]{1,0:T(8,128)S(1)}, u32[]{:S(2)}) copy-start(f32[128,128]{1,0:T(8,128)S(1)} %get-tuple-element.5.prod_ref) | copy-start | bytes 196612
  29.7 0.6 %copy-start.5 = (f32[64,64]{1,0:T(8,128)}, f32[64,64]{1,0:T(8,128)S(1)}, u32[]{:S(2)}) copy-start(f32[64,64]{1,0:T(8,128)S(1)} %get-tuple-element.6.next_in) | copy-start | bytes 49156

commit v2 on v1

--- a/solution.py
+++ b/solution.py
@@ -21,17 +21,26 @@
 
 def gather_kernel(
     n,
-    right_any,
-    diag_any,
-    pr_ref,
-    fin_ref,
-    pl_ref,
-    prhs_ref,
-    prod_ref,
+    ranks_ref,
+    left_hbm,
+    right_hbm,
+    rhs_hbm,
+    pl_hbm,
+    pr_hbm,
+    fin_hbm,
+    prhs_hbm,
+    diag_hbm,
+    nl_ref,
+    nr_ref,
     next_ref,
     buf,
+    left_v,
     right_v,
     diag_v,
+    pl_v,
+    pr_v,
+    fin_v,
+    prhs_v,
     in_sem,
     send_sem,
     recv_sem,
@@ -50,13 +59,20 @@
     def block(zz, ff, gg, cc=core):
         return zz * (2 * side * side) + ff * s1 + gg * s2 + cc
 
-    load_right = pltpu.make_async_copy(right_any, right_v, in_sem.at[0])
-    load_diag = pltpu.make_async_copy(diag_any, diag_v, in_sem.at[1])
-    load_right.start()
-    load_diag.start()
-    half = pr_ref.shape[1]
-    buf[0, me] = jnp.concatenate([pr_ref[...].astype(F32), fin_ref[...]], axis=1)
-    buf[1, me] = jnp.concatenate([pl_ref[...].astype(F32), prhs_ref[...]], axis=1)
+    pairs = (
+        (pr_hbm, pr_v),
+        (fin_hbm, fin_v),
+        (pl_hbm, pl_v),
+        (prhs_hbm, prhs_v),
+        (right_hbm, right_v),
+        (left_hbm, left_v),
+        (rhs_hbm, nr_ref),
+        (diag_hbm, diag_v),
+    )
+    loads = [pltpu.make_async_copy(src, dst, in_sem.at[i]) for i, (src, dst) in enumerate(pairs)]
+    for load in loads:
+        load.start()
+    half = pr_v.shape[1]
 
     def around(digit, size):
         order = sorted(range(1, size), key=lambda d: min(d, size - d))
@@ -72,6 +88,10 @@
     everyone = z_to + f_to + g_to + [partner]
     for peer in everyone:
         pl.semaphore_signal(barrier, inc=1, device_id=(peer,), device_id_type=MESH)
+    for load in loads[:4]:
+        load.wait()
+    buf[0, me] = jnp.concatenate([pr_v[...].astype(F32), fin_v[...]], axis=1)
+    buf[1, me] = jnp.concatenate([pl_v[...].astype(F32), prhs_v[...]], axis=1)
     pl.semaphore_wait(barrier, len(everyone))
 
     sent = []
@@ -143,14 +163,26 @@
 
     rows = n * buf.shape[2]
     solved = buf[0].reshape(rows, 2 * half).astype(BF16)
-    load_right.wait()
+    for load in loads[4:]:
+        load.wait()
     tiles, kmax, width = right_v.shape
-    prod_ref[...] = jnp.dot(right_v[...].reshape(tiles * kmax, width), solved, preferred_element_type=F32)
+    prod = jnp.dot(right_v[...].reshape(tiles * kmax, width), solved, preferred_element_type=F32)
     cross = lax.dot_general(solved, solved, (((0,), (0,)), ((), ())), preferred_element_type=F32)
     at_row = lax.broadcasted_iota(jnp.int32, cross.shape, 0)
     at_lane = lax.broadcasted_iota(jnp.int32, cross.shape, 1)
     weight = jnp.where((at_row < half) & (at_lane >= half), cross, 0.0).astype(BF16)
-    load_diag.wait()
+    chunk = 512 if width % 512 == 0 else width
+    for t in range(tiles):
+        rank = ranks_ref[t]
+        part = prod[t * kmax : (t + 1) * kmax]
+        part = jnp.where(lax.broadcasted_iota(jnp.int32, part.shape, 0) < rank, part, 0.0)
+        coef = part.T.astype(BF16)
+        for w in range(0, width, chunk):
+            left = left_v[t, :, w : w + chunk]
+            keep = lax.broadcasted_iota(jnp.int32, left.shape, 0) < rank
+            out = jnp.dot(coef, jnp.where(keep, left, jnp.zeros_like(left)), preferred_element_type=F32)
+            nl_ref[t, :, w : w + chunk] = out[:half].astype(BF16)
+            nr_ref[t, :, w : w + chunk] = nr_ref[t, :, w : w + chunk] - out[half:]
 
     stage_g(1)
     stage_core(1)
@@ -163,23 +195,6 @@
         c.wait_send()
 
 
-def tile_kernel(ranks_ref, prod_ref, left_ref, rhs_ref, next_in, nl_ref, nr_ref, next_out):
-    t = pl.program_id(0)
-    kmax = left_ref.shape[1]
-    half = nl_ref.shape[1]
-    rank = ranks_ref[t]
-    prod = prod_ref[...]
-    prod = jnp.where(lax.broadcasted_iota(jnp.int32, prod.shape, 0) < rank, prod, 0.0)
-    coef = prod.T.astype(BF16)
-    left = left_ref[0]
-    keep = lax.broadcasted_iota(jnp.int32, left.shape, 0) < rank
-    left_m = jnp.where(keep, left, jnp.zeros_like(left))
-    out = jnp.dot(coef, left_m, preferred_element_type=F32)
-    nl_ref[0] = out[:half].astype(nl_ref.dtype)
-    nr_ref[0] = rhs_ref[0] - out[half:]
-    next_out[...] = next_in[...]
-
-
 def solution(mesh):
     n = mesh.shape["blk"]
 
@@ -187,54 +202,35 @@
         tiles, kmax, width = panel_left.shape
         rows, half = finished.shape
         vmem = pl.BlockSpec(memory_space=pltpu.VMEM)
-        hbm = pl.BlockSpec(memory_space=pl.ANY)
+        hbm = pl.BlockSpec(memory_space=pltpu.HBM)
         deep, side = factors(n)
         steps = (deep - 1) + deep * (side - 1) + deep * side * (side - 1) + deep * side * side
-        prod, nxt = pl.pallas_call(
+        return pl.pallas_call(
             functools.partial(gather_kernel, n),
-            out_shape=(
-                jax.ShapeDtypeStruct((tiles * kmax, 2 * half), F32),
-                jax.ShapeDtypeStruct((rows, half), F32),
-            ),
-            in_specs=[hbm, hbm, vmem, vmem, vmem, vmem],
-            out_specs=(vmem, vmem),
-            scratch_shapes=[
-                pltpu.VMEM((2, n, rows, 2 * half), F32),
-                pltpu.VMEM(panel_right.shape, BF16),
-                pltpu.VMEM(diag_inverse.shape, F32),
-                pltpu.SemaphoreType.DMA((2,)),
-                pltpu.SemaphoreType.DMA((2, steps)),
-                pltpu.SemaphoreType.DMA((2, n)),
-            ],
-            compiler_params=pltpu.CompilerParams(
-                collective_id=0, has_side_effects=True, vmem_limit_bytes=32 * 1024 * 1024
-            ),
-        )(panel_right, diag_inverse, pivot_right, finished, pivot_left, pivot_rhs)
-
-        cut = 2 if width % 256 == 0 else 1
-        chunk = width // cut
-        new_left, new_rhs, next_solution = pl.pallas_call(
-            tile_kernel,
-            grid=(tiles, cut),
             out_shape=(
                 jax.ShapeDtypeStruct((tiles, half, width), BF16),
                 jax.ShapeDtypeStruct((tiles, half, width), F32),
                 jax.ShapeDtypeStruct((rows, half), F32),
             ),
-            in_specs=[
-                pl.BlockSpec(memory_space=pltpu.SMEM),
-                pl.BlockSpec((kmax, 2 * half), lambda t, w: (t, 0)),
-                pl.BlockSpec((1, kmax, chunk), lambda t, w: (t, 0, w)),
-                pl.BlockSpec((1, half, chunk), lambda t, w: (t, 0, w)),
-                pl.BlockSpec((rows, half), lambda t, w: (0, 0)),
+            in_specs=[pl.BlockSpec(memory_space=pltpu.SMEM)] + [hbm] * 8,
+            out_specs=(vmem, vmem, vmem),
+            scratch_shapes=[
+                pltpu.VMEM((2, n, rows, 2 * half), F32),
+                pltpu.VMEM(panel_left.shape, BF16),
+                pltpu.VMEM(panel_right.shape, BF16),
+                pltpu.VMEM(diag_inverse.shape, F32),
+                pltpu.VMEM(pivot_left.shape, BF16),
+                pltpu.VMEM(pivot_right.shape, BF16),
+                pltpu.VMEM(finished.shape, F32),
+                pltpu.VMEM(pivot_rhs.shape, F32),
+                pltpu.SemaphoreType.DMA((8,)),
+                pltpu.SemaphoreType.DMA((2, steps)),
+                pltpu.SemaphoreType.DMA((2, n)),
             ],
-            out_specs=(
-                pl.BlockSpec((1, half, chunk), lambda t, w: (t, 0, w)),
-                pl.BlockSpec((1, half, chunk), lambda t, w: (t, 0, w)),
-                pl.BlockSpec((rows, half), lambda t, w: (0, 0)),
+            compiler_params=pltpu.CompilerParams(
+                collective_id=0, has_side_effects=True, vmem_limit_bytes=67043328
             ),
-        )(ranks, prod, panel_left, rhs, nxt)
-        return new_left, new_rhs, next_solution
+        )(ranks, panel_left, panel_right, rhs, pivot_left, pivot_right, finished, pivot_rhs, diag_inverse)
 
     in_specs = (
         P("blk", None, None),

time: 35 us -> 29.7 us (0.85)
  the two profiles are of different devices: /device:TPU:5 before, /device:TPU:0 now
where the time goes in v2:
time: 29.7 us; the launch traced here: 29.1 us
  Pallas kernels  24.9 us (84%)
  local copies, waits for them, and re-layouts  3.56 us (12%)
  between operations  0.65 us (2%)
    pallas_call x1, Pallas kernels, shards(): pl.pallas_call(functools.partial(gather_kernel, n), out_shape=(jax.ShapeD...  24.9 us
    unnamed x7, local copies, waits for them, and re-layouts  3.56 us

profile of v2, /device:TPU:0, one launch (start us, length us, event | category | flops | bytes accessed | tf_op | source)
XLA Modules:
  0.0 29.1 jit_solution(4927119281306440132)
XLA Ops:
  0.6 24.9 %shard_map.112 = (bf16[2,64,2048]{2,1,0:T(8,128)(2,1)}, f32[2,64,2048]{2,1,0:T(8,128)}, f32[64,64]{1,0:T(8,128)}) custom-call(s32[2]{0:T(128)} %ranks_ref.1, bf16[2,64,2048]{2,1,0:T(8,128)(2,1)} %left_hbm.1, bf16[2,64,2048]{2,1,0:T(8,128)(2,1)} %right_hbm.1, f32[2,64,2048]{2,1,0:T(8,128)} %rhs_hbm.1, bf16[64,64]{1,0:T(8,128)(2,1)} %pl_hbm.1, ...), custom_call_target="tpu_custom_call" | custom-call | tf_op jit(solution)/shard_map/pallas_call | solution.py:208
  25.6 0.0 copy-start
  25.6 2.0 %copy.15 = bf16[2,64,2048]{2,1,0:T(8,128)(2,1)} copy(bf16[2,64,2048]{2,1,0:T(8,128)(2,1)} %get-tuple-element.6) | data formatting | bytes 1048576
  27.5 0.0 copy-done
  27.5 0.0 copy-start.1
  27.5 1.0 %copy.16 = f32[2,64,2048]{2,1,0:T(8,128)} copy(f32[2,64,2048]{2,1,0:T(8,128)S(1)} %copy-done) | data formatting | bytes 2097152
  28.5 0.0 copy-done.1
  28.5 0.6 %copy.17 = f32[64,64]{1,0:T(8,128)} copy(f32[64,64]{1,0:T(8,128)S(1)} %copy-done.1) | data formatting | bytes 32768
Async XLA Ops:
  25.6 2.0 %copy-start = (f32[2,64,2048]{2,1,0:T(8,128)S(1)}, f32[2,64,2048]{2,1,0:T(8,128)}, u32[]{:S(2)}) copy-start(f32[2,64,2048]{2,1,0:T(8,128)} %get-tuple-element.7) | copy-start | bytes 3145732
  27.5 1.0 %copy-start.1 = (f32[64,64]{1,0:T(8,128)S(1)}, f32[64,64]{1,0:T(8,128)}, u32[]{:S(2)}) copy-start(f32[64,64]{1,0:T(8,128)} %get-tuple-element.8) | copy-start | bytes 49156

commit v3 on v2

--- a/solution.py
+++ b/solution.py
@@ -195,6 +195,15 @@
         c.wait_send()
 
 
+def write_kernel(nl_ref, nr_ref, next_ref, nl_out, nr_out, next_out, sem):
+    pairs = ((nr_ref, nr_out), (nl_ref, nl_out), (next_ref, next_out))
+    stores = [pltpu.make_async_copy(src, dst, sem.at[i]) for i, (src, dst) in enumerate(pairs)]
+    for store in stores:
+        store.start()
+    for store in stores:
+        store.wait()
+
+
 def solution(mesh):
     n = mesh.shape["blk"]
 
@@ -205,7 +214,9 @@
         hbm = pl.BlockSpec(memory_space=pltpu.HBM)
         deep, side = factors(n)
         steps = (deep - 1) + deep * (side - 1) + deep * side * (side - 1) + deep * side * side
-        return pl.pallas_call(
+        arrays = (ranks, panel_left, panel_right, rhs, pivot_left, pivot_right, finished, pivot_rhs, diag_inverse)
+        pinned = [pltpu.with_memory_space_constraint(a, pltpu.HBM) for a in arrays]
+        results = pl.pallas_call(
             functools.partial(gather_kernel, n),
             out_shape=(
                 jax.ShapeDtypeStruct((tiles, half, width), BF16),
@@ -228,9 +239,17 @@
                 pltpu.SemaphoreType.DMA((2, n)),
             ],
             compiler_params=pltpu.CompilerParams(
-                collective_id=0, has_side_effects=True, vmem_limit_bytes=67043328
+                collective_id=0, has_side_effects=True, vmem_limit_bytes=40 * 1024 * 1024
             ),
-        )(ranks, panel_left, panel_right, rhs, pivot_left, pivot_right, finished, pivot_rhs, diag_inverse)
+        )(*pinned)
+        return pl.pallas_call(
+            write_kernel,
+            out_shape=tuple(jax.ShapeDtypeStruct(r.shape, r.dtype) for r in results),
+            in_specs=[vmem] * 3,
+            out_specs=(hbm, hbm, hbm),
+            scratch_shapes=[pltpu.SemaphoreType.DMA((3,))],
+            compiler_params=pltpu.CompilerParams(vmem_limit_bytes=4 * 1024 * 1024),
+        )(*results)
 
     in_specs = (
         P("blk", None, None),

time: 29.7 us -> 26.1 us (0.88)
  the two profiles are of different devices: /device:TPU:0 before, /device:TPU:5 now
where the time goes in v3:
time: 26.1 us; the launch traced here: 25.9 us
  Pallas kernels  25.2 us (97%)
  between operations  0.64 us (2%)
    pallas_call x1, Pallas kernels, shards(): pl.pallas_call(functools.partial(gather_kernel, n), out_shape=(jax.ShapeD...  24.1 us
    pallas_call x1, Pallas kernels, shards(): pl.pallas_call(write_kernel, out_shape=tuple((jax.ShapeDtypeStruct(r.shap...  1.17 us

profile of v3, /device:TPU:5, one launch (start us, length us, event | category | flops | bytes accessed | tf_op | source)
XLA Modules:
  0.0 25.9 jit_solution(11287319138701018447)
XLA Ops:
  0.6 24.1 %shard_map.112 = (bf16[2,64,2048]{2,1,0:T(8,128)(2,1)S(1)}, f32[2,64,2048]{2,1,0:T(8,128)S(1)}, f32[64,64]{1,0:T(8,128)S(1)}) custom-call(s32[2]{0:T(128)} %ranks_ref.1, bf16[2,64,2048]{2,1,0:T(8,128)(2,1)} %left_hbm.1, bf16[2,64,2048]{2,1,0:T(8,128)(2,1)} %right_hbm.1, f32[2,64,2048]{2,1,0:T(8,128)} %rhs_hbm.1, bf16[64,64]{1,0:T(8,128)(2,1)} %pl_hbm.1, ...), custom_call_target="tpu_custom_call" | custom-call | tf_op jit(solution)/shard_map/pallas_call | solution.py:219
  24.7 1.2 %shard_map.113 = (bf16[2,64,2048]{2,1,0:T(8,128)(2,1)}, f32[2,64,2048]{2,1,0:T(8,128)}, f32[64,64]{1,0:T(8,128)}) custom-call(bf16[2,64,2048]{2,1,0:T(8,128)(2,1)S(1)} %get-tuple-element.6.nl_ref, f32[2,64,2048]{2,1,0:T(8,128)S(1)} %get-tuple-element.7.nr_ref, f32[64,64]{1,0:T(8,128)S(1)} %get-tuple-element.8.next_ref), custom_call_target="tpu_custom_call" | custom-call | tf_op jit(solution)/shard_map/pallas_call | solution.py:245
